TPU v7x, 32 devices: a whole 2x2x4 slice. The times are simulated.
32 devices in a mesh: dp: 4 (over x, core), row: 2 (over y), col: 4 (over z).
Axes of the slice: x: 2, y: 2, z: 4, core: 2. Of those that a mesh axis runs over, the one named last changes fastest.
Arguments:
- act_in: bfloat16 [4096, 2304], P(('dp', 'row'), 'col'), may hold values from -6 to 6
- cot_out: bfloat16 [4096, 2304], P(('dp', 'row'), 'col'), may hold values from -6 to 6
- w_gate: bfloat16 [2304, 4608], P(('dp', 'row'), 'col'), may hold values from -0.125 to 0.125
- w_up: bfloat16 [2304, 4608], P(('dp', 'row'), 'col'), may hold values from -0.125 to 0.125
- w_down: bfloat16 [4608, 2304], P('col', ('dp', 'row')), may hold values from -0.09375 to 0.09375
Outputs:
- input_grad: bfloat16 [4096, 2304], P(('dp', 'row'), 'col')
- gate_grad: float32 [2304, 4608], P(('dp', 'row'), 'col')
- up_grad: float32 [2304, 4608], P(('dp', 'row'), 'col')
- down_grad: float32 [4608, 2304], P('col', ('dp', 'row'))
All inputs are finite; a program needn't handle non-finite values.
Results may differ from a plain program's by a relative error of at most 0.015.
Values may be sent and summed in bfloat16 or wider, within the bound.
No kernel may reach another device: no remote copies, remote signals or barrier semaphores. Data moves between devices by JAX's collectives and lax.ppermute only.
A program may use at most 128 MiB of HBM per device.

v0:
```python
import math
import jax
import jax.numpy as jnp
from jax import lax
from jax.sharding import PartitionSpec as P

gelu_cubic = 0.044715
gelu_scale = 0.7978845608028654


def gelu_parts(values):
    inner_arg = gelu_scale * (values + gelu_cubic * values * values * values)
    tanh_val = jnp.tanh(inner_arg)
    output = 0.5 * values * (1.0 + tanh_val)
    slope_val = 0.5 * (1.0 + tanh_val) + 0.5 * values * (1.0 - tanh_val * tanh_val) * gelu_scale * (
        1.0 + 3.0 * gelu_cubic * values * values
    )
    return (output, slope_val)


def token_contract(left, right):
    return lax.dot_general(
        left, right, (((0,), (0,)), ((), ())), preferred_element_type=jnp.float32
    )


def body(act_in, cot_out, w_gate, w_up, w_down):
    tok_rows = act_in.shape[0]
    hid_cols = w_gate.shape[1]
    act_full, cot_full = (
        lax.all_gather(act_in, "col", axis=1, tiled=True),
        lax.all_gather(cot_out, "col", axis=1, tiled=True),
    )
    gate_cols, up_cols = (
        lax.all_gather(w_gate, ("dp", "row"), axis=0, tiled=True),
        lax.all_gather(w_up, ("dp", "row"), axis=0, tiled=True),
    )
    gate_pre = jnp.dot(act_full, gate_cols, preferred_element_type=jnp.float32)
    up_pre = jnp.dot(act_full, up_cols, preferred_element_type=jnp.float32)
    cot_block = cot_full
    hidden_grad = lax.dot_general(
        cot_block,
        lax.all_gather(w_down, ("dp", "row"), axis=1, tiled=True),
        (((1,), (1,)), ((), ())),
        preferred_element_type=jnp.float32,
    )
    act_val, slope_val = gelu_parts(gate_pre)
    hidden = (act_val * up_pre).astype(jnp.bfloat16)
    d_gate = (hidden_grad * up_pre * slope_val).astype(jnp.bfloat16)
    d_up = (hidden_grad * act_val).astype(jnp.bfloat16)
    feature_dims = (((1,), (1,)), ((), ()))
    part_sum = lax.dot_general(d_gate, gate_cols, feature_dims, preferred_element_type=jnp.float32)
    part_sum = part_sum + lax.dot_general(
        d_up, up_cols, feature_dims, preferred_element_type=jnp.float32
    )
    rounded = lax.optimization_barrier(part_sum.astype(jnp.bfloat16)).astype(jnp.float32)
    input_grad = lax.psum_scatter(
        rounded.astype(jnp.bfloat16), "col", scatter_dimension=1, tiled=True
    )
    norm_scale = 1.0 / math.sqrt(tok_rows * lax.axis_size(("dp", "row")))
    cot_block = cot_full
    shares = lax.psum_scatter(
        jnp.concatenate(
            [
                token_contract(act_full, d_gate),
                token_contract(act_full, d_up),
                token_contract(cot_block, hidden),
            ],
            axis=1,
        ).astype(jnp.bfloat16),
        ("dp", "row"),
        scatter_dimension=0,
        tiled=True,
    ).astype(jnp.float32)
    gate_grad = shares[:, :hid_cols] * norm_scale
    up_grad = shares[:, hid_cols : 2 * hid_cols] * norm_scale
    down_grad = shares[:, 2 * hid_cols :].T * norm_scale
    return (input_grad, gate_grad, up_grad, down_grad)


def solution(mesh):
    placed = (
        P(("dp", "row"), "col"),
        P(("dp", "row"), "col"),
        P(("dp", "row"), "col"),
        P(("dp", "row"), "col"),
        P("col", ("dp", "row")),
    )
    return jax.shard_map(
        body,
        mesh=mesh,
        in_specs=placed,
        out_specs=(
            P(("dp", "row"), "col"),
            P(("dp", "row"), "col"),
            P(("dp", "row"), "col"),
            P("col", ("dp", "row")),
        ),
        check_vma=False,
    )
```

profile of v0, /device:TPU:0, one launch (start us, length us, event | category | flops | bytes accessed | tf_op | source)
XLA Modules:
  0.0 470.1 jit_solution(8092065288769232010)
XLA Ops:
  10.6 51.7 %all-gather.10.cloned.1.call-done = bf16[512,2304]{0,1:T(8,128)(2,1)} async-done(((bf16[512,576]{0,1:T(8,128)(2,1)}), bf16[512,2304]{0,1:T(8,128)(2,1)}) %all-gather.10.cloned.1.call-update) | async-done | bytes 2359312 | tf_op jit(solution)/shard_map/all_gather | solution.py:31
  62.3 41.9 %all-gather.12.cloned.1.call-done = bf16[2304,1152]{1,0:T(8,128)(2,1)} async-done(((bf16[288,1152]{1,0:T(8,128)(2,1)}), bf16[2304,1152]{1,0:T(8,128)(2,1)}) %all-gather.12.cloned.1.call-update) | async-done | bytes 5308432 | tf_op jit(solution)/shard_map/all_gather | solution.py:36
  104.2 7.9 %fusion.16 = f32[512,1152]{1,0:T(8,128)} fusion(bf16[512,2304]{0,1:T(8,128)(2,1)} %all-gather.10.cloned.1.call-done, bf16[2304,1152]{1,0:T(8,128)(2,1)} %all-gather.12.cloned.1.call-done), kind=kOutput, calls=%fused_computation.29 | convolution fusion | flops 2717908992 | bytes 10027008 | tf_op jit(solution)/shard_map/dot_general | solution.py:39
  112.1 35.3 %all-gather.14.cloned.1.call-done = bf16[2304,1152]{1,0:T(8,128)(2,1)} async-done(((bf16[288,1152]{1,0:T(8,128)(2,1)}), bf16[2304,1152]{1,0:T(8,128)(2,1)}) %all-gather.14.cloned.1.call-update) | async-done | bytes 5308432 | tf_op jit(solution)/shard_map/all_gather | solution.py:35
  147.4 7.2 %fusion.17 = f32[512,1152]{1,0:T(8,128)} fusion(bf16[512,2304]{0,1:T(8,128)(2,1)S(1)} %copy-done, bf16[2304,1152]{1,0:T(8,128)(2,1)} %all-gather.14.cloned.1.call-done), kind=kOutput, calls=%fused_computation.30 | convolution fusion | flops 2717908992 | bytes 10027008 | tf_op jit(solution)/shard_map/dot_general | solution.py:38
  154.6 44.2 %all-gather.6.cloned.1.call-done = bf16[512,2304]{0,1:T(8,128)(2,1)} async-done(((bf16[512,576]{0,1:T(8,128)(2,1)}), bf16[512,2304]{0,1:T(8,128)(2,1)}) %all-gather.6.cloned.1.call-update) | async-done | bytes 2359312 | tf_op jit(solution)/shard_map/all_gather | solution.py:32
  198.8 9.2 %fusion.2 = bf16[2304,1152]{0,1:T(8,128)(2,1)} fusion(bf16[512,2304]{0,1:T(8,128)(2,1)} %all-gather.6.cloned.1.call-done, f32[512,1152]{1,0:T(8,128)} %fusion.16, f32[512,1152]{1,0:T(8,128)} %fusion.17), kind=kOutput, calls=%fused_computation.6 | convolution fusion | flops 2726461440 | bytes 12386304 | tf_op jit(solution)/shard_map/dot_general | solution.py:22
  208.0 32.6 %all-gather.8.cloned.1.call-done = bf16[1152,2304]{0,1:T(8,128)(2,1)} async-done(((bf16[1152,288]{0,1:T(8,128)(2,1)}), bf16[1152,2304]{0,1:T(8,128)(2,1)}) %all-gather.8.cloned.1.call-update) | async-done | bytes 5308432 | tf_op jit(solution)/shard_map/all_gather | solution.py:43
  240.6 9.5 %multiply_convert_fusion.1 = (bf16[512,1152]{1,0:T(8,128)(2,1)S(1)}, bf16[512,1152]{1,0:T(8,128)(2,1)S(1)}) fusion(f32[512,1152]{1,0:T(8,128)} %fusion.17, f32[512,1152]{1,0:T(8,128)} %fusion.16, bf16[512,2304]{0,1:T(8,128)(2,1)} %all-gather.6.cloned.1.call-done, bf16[1152,2304]{0,1:T(8,128)(2,1)} %all-gather.8.cloned.1.call-done), kind=kOutput, calls=%fused_computation.19 | convolution fusion | flops 2731474944 | bytes 14745600 | tf_op jit(solution)/shard_map/dot_general | solution.py:41
  250.1 3.5 fusion.1
  253.6 3.5 fusion
  257.2 23.7 %pad_maximum_fusion = bf16[2304,3456]{0,1:T(8,128)(2,1)} fusion(bf16[2304,1152]{0,1:T(8,128)(2,1)S(1)} %bitcast.28, bf16[2304,1152]{0,1:T(8,128)(2,1)S(1)} %fusion.1, bf16[2304,1152]{0,1:T(8,128)(2,1)S(1)} %fusion), kind=kLoop, calls=%fused_computation | loop fusion | flops 47775744 | bytes 31850496 | tf_op jit(solution)/shard_map/concatenate | solution.py:63
  280.9 20.3 %copy.19 = bf16[2304,3456]{1,0:T(8,128)(2,1)} copy(bf16[2304,3456]{0,1:T(8,128)(2,1)} %pad_maximum_fusion) | data formatting | bytes 31850496
  301.5 1.0 copy-done.2
  302.5 5.7 %fusion.18 = f32[512,2304]{1,0:T(8,128)S(1)} fusion(bf16[512,1152]{1,0:T(8,128)(2,1)S(1)} %copy-done.2, bf16[2304,1152]{1,0:T(8,128)(2,1)} %all-gather.14.cloned.1.call-done), kind=kOutput, calls=%fused_computation.31 | convolution fusion | flops 2717908992 | bytes 11206656 | tf_op jit(solution)/shard_map/dot_general | solution.py:52
  308.3 7.1 %fusion.3 = bf16[512,2304]{1,0:T(8,128)(2,1)S(1)} fusion(f32[512,2304]{1,0:T(8,128)S(1)} %fusion.18, bf16[512,1152]{1,0:T(8,128)(2,1)S(1)} %get-tuple-element.15, bf16[2304,1152]{1,0:T(8,128)(2,1)} %all-gather.12.cloned.1.call-done), kind=kOutput, calls=%fused_computation.8 | convolution fusion | flops 2720268288 | bytes 13565952 | tf_op jit(solution)/shard_map/dot_general | solution.py:53
  315.4 2.5 copy.17
  317.9 94.8 %reduce-scatter.9.cloned.1.call-done = bf16[288,3456]{1,0:T(8,128)(2,1)} async-done(((bf16[2304,3456]{1,0:T(8,128)(2,1)}), bf16[288,3456]{1,0:T(8,128)(2,1)}) %reduce-scatter.9.cloned.1.call-update) | async-done | bytes 1990672
  412.7 3.0 copy.20
  416.0 1.6 fusion.11
  417.6 3.0 copy.16
  420.6 1.6 copy.15
  422.2 1.6 copy.14
  423.8 39.5 %reduce-scatter.7.cloned.1.call-done = bf16[576,512]{1,0:T(8,128)(2,1)} async-done(((bf16[2304,512]{1,0:T(8,128)(2,1)}), bf16[576,512]{1,0:T(8,128)(2,1)}) %reduce-scatter.7.cloned.1.call-update) | async-done | bytes 589840
  (25 shorter events, 4.0 us)
Async XLA Ops:
  7.2 55.1 %all-gather.10.cloned.1.call-start = ((), (), s32[]{:S(2)}) async-start(), calls=%async_computation.4 | async-start | bytes 2949120 | tf_op jit(solution)/shard_map/all_gather | solution.py:31
  7.9 96.3 %all-gather.12.cloned.1.call-start = ((), (), s32[]{:S(2)}) async-start(), calls=%async_computation.5 | async-start | bytes 5971968 | tf_op jit(solution)/shard_map/all_gather | solution.py:36
  8.6 138.7 %all-gather.14.cloned.1.call-start = ((), (), s32[]{:S(2)}) async-start(), calls=%async_computation.6 | async-start | bytes 5971968 | tf_op jit(solution)/shard_map/all_gather | solution.py:35
  9.4 189.4 %all-gather.6.cloned.1.call-start = ((), (), s32[]{:S(2)}) async-start(), calls=%async_computation.2 | async-start | bytes 2949120 | tf_op jit(solution)/shard_map/all_gather | solution.py:32
  10.0 230.6 %all-gather.8.cloned.1.call-start = ((), (), s32[]{:S(2)}) async-start(), calls=%async_computation.3 | async-start | bytes 5971968 | tf_op jit(solution)/shard_map/all_gather | solution.py:43
  10.5 402.1 %reduce-scatter.9.cloned.1.call-start = ((), (), s32[]{:S(2)}) async-start(), calls=%async_computation.8 | async-start | bytes 17915904
  62.3 85.1 %copy-start = (bf16[512,2304]{0,1:T(8,128)(2,1)S(1)}, bf16[512,2304]{0,1:T(8,128)(2,1)}, u32[]{:S(2)}) copy-start(bf16[512,2304]{0,1:T(8,128)(2,1)} %all-gather.10.cloned.1.call-done) | copy-start | bytes 7077892
  250.1 3.6 copy-start.1
  250.1 7.1 %slice-start = ((s8[5308416]{0:T(1024)(128)(4,1)}), s8[4194304]{0:T(1024)(128)(4,1)S(1)}, s32[]{:S(2)}) async-start(s8[5308416]{0:T(1024)(128)(4,1)} %bitcast.27), calls=%async_computation.9 | async-start | bytes 8388608
  253.6 3.6 slice-start.1
  301.2 1.3 copy-start.2
  301.3 162.0 %reduce-scatter.7.cloned.1.call-start = ((), (), s32[]{:S(2)}) async-start(), calls=%async_computation.7 | async-start | bytes 2949120
Sparse Core Ops, SparseCore 0:
  9.5 52.6 all-gather.9
  64.2 40.0 all-gather.11
  106.1 41.2 all-gather.13
  148.8 49.9 all-gather.5
  200.5 40.0 all-gather.7
  301.4 111.2 reduce-scatter.8
  415.5 47.6 reduce-scatter.6
where the time goes:
time: 471 us; the launch traced here: 470 us
  waiting for transfers between devices  343 us (73%)
  matrix products  53.6 us (11%)
  local copies, waits for them, and re-layouts  33 us (7%)
  other arithmetic  25.6 us (5%)
  between operations  14.2 us (3%)
    unnamed x9, waiting for transfers between devices  137 us
    all_gather x1, waiting for transfers between devices, body(): lax.all_gather(act_in, 'col', axis=1, tiled=True)  51.7 us
    all_gather x1, waiting for transfers between devices, body(): lax.all_gather(cot_out, 'col', axis=1, tiled=True)  44.2 us
    all_gather x1, waiting for transfers between devices, body(): lax.all_gather(w_up, ('dp', 'row'), axis=0, tiled=True)  41.9 us
    all_gather x1, waiting for transfers between devices, body(): lax.all_gather(w_gate, ('dp', 'row'), axis=0, tiled=True)  35.3 us
    unnamed x16, local copies, waits for them, and re-layouts  33 us
    all_gather x1, waiting for transfers between devices, body(): lax.all_gather(w_down, ('dp', 'row'), axis=1, tiled=True)  32.6 us
    concatenate x1, other arithmetic, body(): jnp.concatenate([token_contract(act_full, d_gate), token_contract(act_ful...  23.7 us
  transfers between devices with their start and end apart: 7, of which 7 were waited for; matrix products, arithmetic and copies ran while one was open for 11% of the time, Pallas kernels for 0%

commit v1 on v0

--- a/solution.py
+++ b/solution.py
@@ -6,6 +6,18 @@
 
 gelu_cubic = 0.044715
 gelu_scale = 0.7978845608028654
+
+
+def collect(x, axis, dim):
+    ways, here, hop = (lax.axis_size(axis), lax.axis_index(axis), x.shape[dim])
+    line, have = (x, 1)
+    while have < ways:
+        line = jnp.concatenate(
+            [line, lax.ppermute(line, axis, [(d, (d - have) % ways) for d in range(ways)])],
+            axis=dim,
+        )
+        have = 2 * have
+    return jnp.roll(line, here * hop, axis=dim)
 
 
 def gelu_parts(values):
@@ -40,7 +52,7 @@
     cot_block = cot_full
     hidden_grad = lax.dot_general(
         cot_block,
-        lax.all_gather(w_down, ("dp", "row"), axis=1, tiled=True),
+        collect(w_down, ("dp", "row"), 1),
         (((1,), (1,)), ((), ())),
         preferred_element_type=jnp.float32,
     )

time: 471 us -> 453 us (0.962)
  waiting for transfers between devices: 343 us -> 310 us
  local copies, waits for them, and re-layouts: 33 us -> 46.2 us
  matrix products: 53.6 us -> 48 us
  starting transfers between devices: 0.49 us -> 5.65 us
    ppermute x0 -> x3, waiting for transfers between devices: none -> 108 us  [collect(): lax.ppermute(line, axis, [(d, (d - have) % ways) for d in range(ways)])]
    all_gather x1, waiting for transfers between devices: 51.7 us -> 0.01 us  [body(): lax.all_gather(act_in, 'col', axis=1, tiled=True)]
    all_gather x1, waiting for transfers between devices: 41.9 us -> 0.01 us  [body(): lax.all_gather(w_up, ('dp', 'row'), axis=0, tiled=True)]
    all_gather x1 -> x0, waiting for transfers between devices: 32.6 us -> none  [body(): lax.all_gather(w_down, ('dp', 'row'), axis=1, tiled=True)]
    all_gather x1, waiting for transfers between devices: 35.3 us -> 22.7 us  [body(): lax.all_gather(w_gate, ('dp', 'row'), axis=0, tiled=True)]
    unnamed x16 -> x27, local copies, waits for them, and re-layouts: 33 us -> 42.5 us
    ppermute x0 -> x3, starting transfers between devices: none -> 5.19 us  [collect(): lax.ppermute(line, axis, [(d, (d - have) % ways) for d in range(ways)])]
    unnamed x9 -> x8, waiting for transfers between devices: 137 us -> 135 us
  transfers between devices with their start and end apart: 7 -> 9, of which waited for: 7 -> 7; matrix products, arithmetic and copies ran while one was open for 11% -> 12% of each run, Pallas kernels for 0% -> 0%
where the time goes in v1:
time: 453 us; the launch traced here: 452 us
  waiting for transfers between devices  310 us (68%)
  matrix products  48 us (11%)
  local copies, waits for them, and re-layouts  46.2 us (10%)
  other arithmetic  27.4 us (6%)
  between operations  14.3 us (3%)
  starting transfers between devices  5.65 us (1%)
    unnamed x8, waiting for transfers between devices  135 us
    ppermute x3, waiting for transfers between devices, collect(): lax.ppermute(line, axis, [(d, (d - have) % ways) for d in range(ways)])  108 us
    all_gather x1, waiting for transfers between devices, body(): lax.all_gather(cot_out, 'col', axis=1, tiled=True)  44.6 us
    unnamed x27, local copies, waits for them, and re-layouts  42.5 us
    concatenate x1, other arithmetic, body(): jnp.concatenate([token_contract(act_full, d_gate), token_contract(act_ful...  23.7 us
    all_gather x1, waiting for transfers between devices, body(): lax.all_gather(w_gate, ('dp', 'row'), axis=0, tiled=True)  22.7 us
    dot_general x3, matrix products, token_contract(): lax.dot_general(left, right, (((0,), (0,)), ((), ())), preferred_element_...  13.1 us
  transfers between devices with their start and end apart: 9, of which 7 were waited for; matrix products, arithmetic and copies ran while one was open for 12% of the time, Pallas kernels for 0%

profile of v1, /device:TPU:0, one launch (start us, length us, event | category | flops | bytes accessed | tf_op | source)
XLA Modules:
  0.0 451.6 jit_solution(10420995049833482231)
XLA Ops:
  9.4 3.4 collective-permute-start
  12.9 14.8 %collective-permute-done = bf16[1152,288]{0,1:T(8,128)(2,1)S(1)} collective-permute-done((bf16[1152,288]{0,1:T(8,128)(2,1)}, bf16[1152,288]{0,1:T(8,128)(2,1)S(1)}, u32[]{:S(2)}, u32[]{:S(2)}) %collective-permute-start) | collective-permute-done | bytes 663584 | tf_op jit(solution)/shard_map/ppermute | solution.py:16
  28.9 15.3 %collective-permute-done.1 = bf16[1152,576]{0,1:T(8,128)(2,1)S(1)} collective-permute-done((bf16[1152,576]{0,1:T(8,128)(2,1)S(1)}, bf16[1152,576]{0,1:T(8,128)(2,1)S(1)}, u32[]{:S(2)}, u32[]{:S(2)}) %collective-permute-start.1) | collective-permute-done | bytes 1327136 | tf_op jit(solution)/shard_map/ppermute | solution.py:16
  44.2 1.7 pad_maximum_fusion.1
  49.6 78.1 %collective-permute-done.2 = bf16[1152,1152]{0,1:T(8,128)(2,1)} collective-permute-done((bf16[1152,1152]{0,1:T(8,128)(2,1)}, bf16[1152,1152]{0,1:T(8,128)(2,1)}, u32[]{:S(2)}, u32[]{:S(2)}) %collective-permute-start.2) | collective-permute-done | bytes 2654240 | tf_op jit(solution)/shard_map/ppermute | solution.py:16
  127.7 3.5 constant_dynamic-update-slice_fusion.4
  134.2 3.7 constant_dynamic-update-slice_fusion
  137.9 7.8 %fusion.22 = f32[512,1152]{0,1:T(8,128)} fusion(bf16[512,2304]{0,1:T(8,128)(2,1)} %all-gather.7.cloned.1.call-done, bf16[2304,1152]{1,0:T(8,128)(2,1)} %all-gather.9.cloned.1.call-done), kind=kOutput, calls=%fused_computation.43 | convolution fusion | flops 2717908992 | bytes 10027008 | tf_op jit(solution)/shard_map/dot_general | solution.py:51
  145.7 22.7 %all-gather.11.cloned.1.call-done = bf16[2304,1152]{1,0:T(8,128)(2,1)} async-done(((bf16[288,1152]{1,0:T(8,128)(2,1)}), bf16[2304,1152]{1,0:T(8,128)(2,1)}) %all-gather.11.cloned.1.call-update) | async-done | bytes 5308432 | tf_op jit(solution)/shard_map/all_gather | solution.py:47
  168.4 6.8 %fusion.23 = f32[512,1152]{0,1:T(8,128)} fusion(bf16[512,2304]{0,1:T(8,128)(2,1)S(1)} %copy-done.1, bf16[2304,1152]{1,0:T(8,128)(2,1)} %all-gather.11.cloned.1.call-done), kind=kOutput, calls=%fused_computation.44 | convolution fusion | flops 2717908992 | bytes 10027008 | tf_op jit(solution)/shard_map/dot_general | solution.py:50
  175.3 44.6 %all-gather.5.cloned.1.call-done = bf16[512,2304]{0,1:T(8,128)(2,1)} async-done(((bf16[512,576]{0,1:T(8,128)(2,1)}), bf16[512,2304]{0,1:T(8,128)(2,1)}) %all-gather.5.cloned.1.call-update) | async-done | bytes 2359312 | tf_op jit(solution)/shard_map/all_gather | solution.py:44
  219.8 6.7 %fusion.2 = bf16[2304,1152]{0,1:T(8,128)(2,1)S(1)} fusion(bf16[512,2304]{0,1:T(8,128)(2,1)} %all-gather.5.cloned.1.call-done, f32[512,1152]{0,1:T(8,128)} %fusion.22, f32[512,1152]{0,1:T(8,128)} %fusion.23), kind=kOutput, calls=%fused_computation.6 | convolution fusion | flops 2726461440 | bytes 12386304 | tf_op jit(solution)/shard_map/dot_general | solution.py:34
  226.6 7.2 %multiply_convert_fusion.1 = (bf16[512,1152]{0,1:T(8,128)(2,1)S(1)}, bf16[512,1152]{0,1:T(8,128)(2,1)S(1)}) fusion(f32[512,1152]{0,1:T(8,128)S(1)} %copy-done.4, f32[512,1152]{0,1:T(8,128)S(1)} %copy-done.3, bf16[512,2304]{0,1:T(8,128)(2,1)S(1)} %copy-done.2, bf16[1152,4608]{0,1:T(8,128)(2,1)} %constant_dynamic-update-slice_fusion, s32[]{:T(128)S(6)} %select_n.14), kind=kOutput, calls=%fused_computation.23 | convolution fusion | flops 2731474944 | bytes 14745604 | tf_op jit(solution)/shard_map/dot_general | solution.py:53
  233.8 3.2 fusion
  237.0 3.2 fusion.1
  240.2 23.7 %pad_maximum_fusion = bf16[2304,3456]{0,1:T(8,128)(2,1)} fusion(bf16[2304,1152]{0,1:T(8,128)(2,1)S(1)} %fusion.2, bf16[2304,1152]{0,1:T(8,128)(2,1)S(1)} %fusion.1, bf16[2304,1152]{0,1:T(8,128)(2,1)S(1)} %fusion), kind=kLoop, calls=%fused_computation | loop fusion | flops 47775744 | bytes 31850496 | tf_op jit(solution)/shard_map/concatenate | solution.py:75
  263.9 20.3 %copy.39 = bf16[2304,3456]{1,0:T(8,128)(2,1)} copy(bf16[2304,3456]{0,1:T(8,128)(2,1)} %pad_maximum_fusion) | data formatting | bytes 31850496
  285.5 5.8 %fusion.24 = f32[512,2304]{1,0:T(8,128)S(1)} fusion(bf16[512,1152]{0,1:T(8,128)(2,1)S(1)} %copy-done.6, bf16[2304,1152]{1,0:T(8,128)(2,1)} %all-gather.11.cloned.1.call-done), kind=kOutput, calls=%fused_computation.45 | convolution fusion | flops 2717908992 | bytes 11206656 | tf_op jit(solution)/shard_map/dot_general | solution.py:64
  291.3 7.3 %fusion.5 = bf16[512,2304]{1,0:T(8,128)(2,1)S(1)} fusion(f32[512,2304]{1,0:T(8,128)S(1)} %fusion.24, bf16[512,1152]{0,1:T(8,128)(2,1)S(1)} %get-tuple-element.15, bf16[2304,1152]{1,0:T(8,128)(2,1)} %all-gather.9.cloned.1.call-done), kind=kOutput, calls=%fused_computation.10 | convolution fusion | flops 2720268288 | bytes 13565952 | tf_op jit(solution)/shard_map/dot_general | solution.py:65
  298.5 2.5 copy.37
  301.1 93.2 %reduce-scatter.9.cloned.1.call-done = bf16[288,3456]{1,0:T(8,128)(2,1)} async-done(((bf16[2304,3456]{1,0:T(8,128)(2,1)}), bf16[288,3456]{1,0:T(8,128)(2,1)}) %reduce-scatter.9.cloned.1.call-update) | async-done | bytes 1990672
  394.3 3.0 copy.40
  399.2 3.0 copy.32
  405.4 39.3 %reduce-scatter.7.cloned.1.call-done = bf16[576,512]{1,0:T(8,128)(2,1)} async-done(((bf16[2304,512]{1,0:T(8,128)(2,1)}), bf16[576,512]{1,0:T(8,128)(2,1)}) %reduce-scatter.7.cloned.1.call-update) | async-done | bytes 589840
  (41 shorter events, 16.5 us)
Async XLA Ops:
  7.2 20.5 %copy-start = (bf16[1152,288]{0,1:T(8,128)(2,1)S(1)}, bf16[1152,288]{0,1:T(8,128)(2,1)}, u32[]{:S(2)}) copy-start(bf16[1152,288]{0,1:T(8,128)(2,1)} %param.9) | copy-start | bytes 1990660
  7.2 130.7 %all-gather.7.cloned.1.call-start = ((), (), s32[]{:S(2)}) async-start(), calls=%async_computation.3 | async-start | bytes 2949120 | tf_op jit(solution)/shard_map/all_gather | solution.py:43
  7.9 130.0 %all-gather.9.cloned.1.call-start = ((), (), s32[]{:S(2)}) async-start(), calls=%async_computation.4 | async-start | bytes 5971968 | tf_op jit(solution)/shard_map/all_gather | solution.py:48
  8.7 159.7 %all-gather.11.cloned.1.call-start = ((), (), s32[]{:S(2)}) async-start(), calls=%async_computation.5 | async-start | bytes 5971968 | tf_op jit(solution)/shard_map/all_gather | solution.py:47
  9.4 210.4 %all-gather.5.cloned.1.call-start = ((), (), s32[]{:S(2)}) async-start(), calls=%async_computation.2 | async-start | bytes 2949120 | tf_op jit(solution)/shard_map/all_gather | solution.py:44
  9.4 18.2 %collective-permute-start = (bf16[1152,288]{0,1:T(8,128)(2,1)}, bf16[1152,288]{0,1:T(8,128)(2,1)S(1)}, u32[]{:S(2)}, u32[]{:S(2)}) collective-permute-start(bf16[1152,288]{0,1:T(8,128)(2,1)} %param.9), channel_id=1, source_target_pairs={{0,28},{4,0},{8,4},{12,8},{16,12},{20,16},{24,20},{28,24},{1,29},{... | collective-permute-start | bytes 1990664 | tf_op jit(solution)/shard_map/ppermute | solution.py:16
  27.7 16.5 %collective-permute-start.1 = (bf16[1152,576]{0,1:T(8,128)(2,1)S(1)}, bf16[1152,576]{0,1:T(8,128)(2,1)S(1)}, u32[]{:S(2)}, u32[]{:S(2)}) collective-permute-start(bf16[1152,576]{0,1:T(8,128)(2,1)S(1)} %pad_maximum_fusion.2), channel_id=1, source_target_pairs={{0,24},{4,28},{8,0},{12,4},{16,8},{20,12},{24,16},{28,20},{1,25},{... | collective-permute-start | bytes 3981320 | tf_op jit(solution)/shard_map/ppermute | solution.py:16
  45.9 81.8 %collective-permute-start.2 = (bf16[1152,1152]{0,1:T(8,128)(2,1)}, bf16[1152,1152]{0,1:T(8,128)(2,1)}, u32[]{:S(2)}, u32[]{:S(2)}) collective-permute-start(bf16[1152,1152]{0,1:T(8,128)(2,1)} %pad_maximum_fusion.1), channel_id=1, source_target_pairs={{0,16},{4,20},{8,24},{12,28},{16,0},{20,4},{24,8},{28,12},{1,17},{... | collective-permute-start | bytes 7962632 | tf_op jit(solution)/shard_map/ppermute | solution.py:16
  46.5 347.8 %reduce-scatter.9.cloned.1.call-start = ((), (), s32[]{:S(2)}) async-start(), calls=%async_computation.7 | async-start | bytes 17915904
  137.9 30.5 %copy-start.1 = (bf16[512,2304]{0,1:T(8,128)(2,1)S(1)}, bf16[512,2304]{0,1:T(8,128)(2,1)}, u32[]{:S(2)}) copy-start(bf16[512,2304]{0,1:T(8,128)(2,1)} %all-gather.7.cloned.1.call-done) | copy-start | bytes 7077892
  219.8 6.7 %copy-start.2 = (bf16[512,2304]{0,1:T(8,128)(2,1)S(1)}, bf16[512,2304]{0,1:T(8,128)(2,1)}, u32[]{:S(2)}) copy-start(bf16[512,2304]{0,1:T(8,128)(2,1)} %all-gather.5.cloned.1.call-done) | copy-start | bytes 7077892
  219.8 6.7 %copy-start.3 = (f32[512,1152]{0,1:T(8,128)S(1)}, f32[512,1152]{0,1:T(8,128)}, u32[]{:S(2)}) copy-start(f32[512,1152]{0,1:T(8,128)} %fusion.22) | copy-start | bytes 7077892
  219.8 6.7 %copy-start.4 = (f32[512,1152]{0,1:T(8,128)S(1)}, f32[512,1152]{0,1:T(8,128)}, u32[]{:S(2)}) copy-start(f32[512,1152]{0,1:T(8,128)} %fusion.23) | copy-start | bytes 7077892
  233.8 3.2 copy-start.5
  284.2 1.3 copy-start.6
  284.3 160.5 %reduce-scatter.7.cloned.1.call-start = ((), (), s32[]{:S(2)}) async-start(), calls=%async_computation.6 | async-start | bytes 2949120
Sparse Core Ops, SparseCore 0:
  9.5 52.6 all-gather.6
  64.2 61.0 all-gather.8
  127.1 41.2 all-gather.10
  169.8 49.9 all-gather.4
  284.4 109.8 reduce-scatter.8
  397.0 47.6 reduce-scatter.6
